TPU v7x, 256 devices: a whole 4x4x8 slice. The times are simulated.
256 devices in a mesh: row: 8 (over y, x_hi), theta: 4 (over x_lo, core), gz: 8 (over z).
Axes of the slice: x: 4 (x_hi: 2, x_lo: 2; x = x_hi * 2 + x_lo), y: 4, z: 8, core: 2. Of those that a mesh axis runs over, the one named last changes fastest.
Arguments:
- state_start: float32 [6, 32, 256, 1024], P(None, 'row', 'gz', 'theta'), may hold values from -1.2 to 1.2
- state_section: float32 [6, 32, 256, 1024], P(None, 'row', 'gz', 'theta'), may hold values from -1.5 to 4, as said below
- phase: int32 [32, 256, 1024], P('row', 'gz', 'theta'), may hold values 0 or 1
- cutoff: int32 [4], replicated, may hold values from 1 to 63
Outputs:
- state_next: float32 [6, 32, 256, 1024], P(None, 'row', 'gz', 'theta')
Inputs may be any that keep to these rules, and one draw needn't show every extreme that they name: `state_section`: channel 0 (density) lies in 0.5 to 2.0, channels 1 to 3 (momenta) in -1.5 to 1.5, channel 4 (total energy) in 2.5 to 4.0, channel 5 (jet mass density) in 0 to 1.0.
All inputs are finite; a program needn't handle non-finite values. No bound on the sum of `phase` on one device may be relied on, other than what follows from the above.
Results may differ from a plain program's by a relative error of at most 0.0003.
Values sent between devices are 32-bit elements; how exact they have to be, the bound alone decides.
No kernel may reach another device: no remote copies, remote signals or barrier semaphores. Data moves between devices by JAX's collectives and lax.ppermute only.
A program may use at most 64 MiB of HBM per device.

v0:
```python
import math

import jax
import jax.numpy as jnp
from jax import lax
from jax.sharding import PartitionSpec as P

NT = 1024
KMODES = 64


split_speed = 10.0
time_step = 0.05
weno_epsilon = 1e-06
liquid_ratio = 4.4
gas_ratio = 1.4
liquid_stiffness = 0.6


def from_everyone(x, axis):
    copies = jnp.broadcast_to(x, (lax.axis_size(axis), *x.shape))
    return lax.all_to_all(copies, axis, split_axis=0, concat_axis=0, tiled=True)


def of_everyone(x, axis):
    everything = from_everyone(x, axis)
    return jnp.sum(everything, axis=0)


def passed_along(value, axis, steps):
    count = lax.axis_size(axis)
    pairs = [(source, (source + steps) % count) for source in range(count)]
    return lax.ppermute(value, axis, pairs)


def padded_2(x, sides, width):
    edges = {}
    for axis, dim in sides:
        peers, length = (lax.axis_size(axis), x.shape[dim])
        up = [(i, (i + 1) % peers) for i in range(peers)]
        last = lax.slice_in_dim(x, length - width, length, axis=dim)
        first = lax.slice_in_dim(x, 0, width, axis=dim)
        edges[dim] = (
            lax.ppermute(last, axis, up),
            lax.ppermute(first, axis, [(b, a) for a, b in up]),
        )
    done = []
    for _, dim in sides:
        low, high = edges[dim]
        around = [(width, width) if d in done else (0, 0) for d in range(x.ndim)]
        x = jnp.concatenate([jnp.pad(low, around), x, jnp.pad(high, around)], axis=dim)
        done.append(dim)
    return x


def pressure_of(state, phase):
    density = state[0]
    kinetic = 0.5 * (state[1] * state[1] + state[2] * state[2] + state[3] * state[3]) / density
    liquid = phase == 1
    heat_ratio = jnp.where(liquid, liquid_ratio, gas_ratio)
    stiffness = jnp.where(liquid, liquid_stiffness, 0.0)
    return (heat_ratio - 1.0) * (state[4] - kinetic) - heat_ratio * stiffness


def weno_face(far_left, near_left, centre, near_right, far_right):
    smooth_left = (
        13.0 / 12.0 * (far_left - 2.0 * near_left + centre) ** 2
        + 0.25 * (far_left - 4.0 * near_left + 3.0 * centre) ** 2
    )
    smooth_mid = (
        13.0 / 12.0 * (near_left - 2.0 * centre + near_right) ** 2
        + 0.25 * (near_left - near_right) ** 2
    )
    smooth_right = (
        13.0 / 12.0 * (centre - 2.0 * near_right + far_right) ** 2
        + 0.25 * (3.0 * centre - 4.0 * near_right + far_right) ** 2
    )
    weight_left = 0.1 / (weno_epsilon + smooth_left) ** 2
    weight_mid = 0.6 / (weno_epsilon + smooth_mid) ** 2
    weight_right = 0.3 / (weno_epsilon + smooth_right) ** 2
    weight_sum = weight_left + weight_mid + weight_right
    value_left = (2.0 * far_left - 7.0 * near_left + 11.0 * centre) / 6.0
    value_mid = (-near_left + 5.0 * centre + 2.0 * near_right) / 6.0
    value_right = (2.0 * centre + 5.0 * near_right - far_right) / 6.0
    return (
        weight_left * value_left + weight_mid * value_mid + weight_right * value_right
    ) / weight_sum


def face_fluxes(padded_line, array_axis, component):
    density = padded_line[0]
    velocity = padded_line[component] / density
    pressure_field = padded_line[6]
    conserved = padded_line[:6]
    flux_rows = [conserved[channel] * velocity for channel in range(6)]
    flux_rows[component] = flux_rows[component] + pressure_field
    flux_rows[4] = flux_rows[4] + pressure_field * velocity
    physical = jnp.stack(flux_rows)
    upward = 0.5 * (physical + split_speed * conserved)
    downward = 0.5 * (physical - split_speed * conserved)
    face_count = padded_line.shape[array_axis] - 5

    def shifted(values, offset):
        return lax.slice_in_dim(values, offset, offset + face_count, axis=array_axis)

    upwind_part = weno_face(
        shifted(upward, 0),
        shifted(upward, 1),
        shifted(upward, 2),
        shifted(upward, 3),
        shifted(upward, 4),
    )
    downwind_part = weno_face(
        shifted(downward, 5),
        shifted(downward, 4),
        shifted(downward, 3),
        shifted(downward, 2),
        shifted(downward, 1),
    )
    return upwind_part + downwind_part


def tendency(centre_cells, radial_line, axial_line, azimuth_line, cycle_start):
    cycle_count = centre_cells.shape[1]
    radial_flux = face_fluxes(radial_line, 1, 1)
    axial_flux = face_fluxes(axial_line, 2, 3)
    azimuth_flux = face_fluxes(azimuth_line, 3, 2)
    cycle_index = (cycle_start + lax.iota(jnp.int32, cycle_count + 1)).astype(centre_cells.dtype)
    face_radius = cycle_index[None, :, None, None]
    cell_radius = face_radius[:, :-1] + 0.5
    weighted = face_radius * radial_flux
    div_radial = (weighted[:, 1:] - weighted[:, :-1]) / cell_radius
    div_axial = axial_flux[:, :, 1:] - axial_flux[:, :, :-1]
    angle_step = 2.0 * math.pi / NT
    div_azimuth = (azimuth_flux[..., 1:] - azimuth_flux[..., :-1]) / (cell_radius * angle_step)
    density = centre_cells[0]
    swirl_speed = centre_cells[2] / density
    radius = cell_radius[0]
    source_radial = (centre_cells[2] * swirl_speed + centre_cells[6]) / radius
    source_swirl = -centre_cells[1] * swirl_speed / radius
    zero_field = jnp.zeros_like(density)
    source = jnp.stack(
        [zero_field, source_radial, source_swirl, zero_field, zero_field, zero_field]
    )
    return source - div_radial - div_axial - div_azimuth


def across_axis(partner):
    sign_flip = jnp.array([1.0, -1.0, -1.0, 1.0, 1.0, 1.0, 1.0], partner.dtype)[:, None, None, None]
    return partner[:, ::-1] * sign_flip


def build_table(positions, mode_count, length):
    orders = lax.iota(jnp.int32, mode_count)
    phases = positions[:, None] * orders[None, :] % length
    angles = phases.astype(jnp.float32) * (2.0 * math.pi / length)
    return jnp.concatenate([jnp.cos(angles), jnp.sin(angles)], 1)


def cycle_weights(cutoff, mode_count, length):
    orders = lax.iota(jnp.int32, mode_count)
    mode_scale = jnp.where(orders == 0, 1.0 / length, 2.0 / length)
    kept_modes = orders[None, :] <= cutoff[:, None]
    weight_half = jnp.where(kept_modes, mode_scale[None, :], 0.0)
    return jnp.concatenate([weight_half, weight_half], 1)


def apply_filter(cycle_block, weights, theta_id):
    local_theta = cycle_block.shape[3]
    positions = theta_id * local_theta + lax.iota(jnp.int32, local_theta)
    fourier_table = build_table(positions, KMODES, NT)
    coefficients = jnp.einsum(
        "vizt,tk->vizk", cycle_block, fourier_table, precision=lax.Precision.HIGHEST
    )
    coefficients = of_everyone(coefficients, "theta")
    coefficients = coefficients * weights[None, :, None, :]
    return jnp.einsum("vizk,tk->vizt", coefficients, fourier_table, precision=lax.Precision.HIGHEST)


def shards(state_start, state_section, phase, cutoff):
    row_count = lax.axis_size("row")
    row_id = lax.axis_index("row")
    theta_count = lax.axis_size("theta")
    theta_id = lax.axis_index("theta")
    cycle_count = state_section.shape[1]
    filtered_count = cutoff.shape[0]
    pressure_field = pressure_of(state_section, phase)
    fields = jnp.concatenate([state_section, pressure_field[None]], 0)
    partner = passed_along(fields[:, 0:3], "theta", theta_count // 2)
    mirror = across_axis(partner)
    outer_rim = jnp.repeat(fields[:, -1:], 3, axis=1)
    padded = padded_2(fields, (("row", 1), ("theta", 3), ("gz", 2)), 3)
    radial_line = padded[:, :, 3:-3, 3:-3]
    axial_line = padded[:, 3:-3, :, 3:-3]
    azimuth_line = padded[:, 3:-3, 3:-3, :]
    lower_rim = jnp.where(row_id == 0, mirror, radial_line[:, :3])
    upper_rim = jnp.where(row_id == row_count - 1, outer_rim, radial_line[:, -3:])
    radial_line = jnp.concatenate([lower_rim, fields, upper_rim], 1)
    tendencies = tendency(fields, radial_line, axial_line, azimuth_line, row_id * cycle_count)
    advanced = 0.75 * state_start + 0.25 * (state_section + time_step * tendencies)
    weights = cycle_weights(cutoff, KMODES, NT)
    filtered = apply_filter(advanced, weights, theta_id)
    inner_next = jnp.where(row_id == 0, filtered, advanced)
    return jnp.concatenate([inner_next, advanced[:, filtered_count:]], 1)


def solution(mesh):
    in_specs = (
        P(None, "row", "gz", "theta"),
        P(None, "row", "gz", "theta"),
        P("row", "gz", "theta"),
        P(),
    )
    out_specs = P(None, "row", "gz", "theta")
    return jax.shard_map(shards, mesh=mesh, in_specs=in_specs, out_specs=out_specs, check_vma=False)
```

profile of v0, /device:TPU:1, one launch (start us, length us, event | category | flops | bytes accessed | tf_op | source)
XLA Modules:
  0.0 109.0 jit_solution(15044057462193722881)
XLA Ops:
  0.0 1.4 %bitcast_dynamic-update-slice_fusion = (f32[6,4,32,256]{3,2,1,0:T(8,128)S(1)}, f32[4,32,256]{2,1,0:T(8,128)S(1)}) fusion(f32[6,4,32,256]{3,2,1,0:T(8,128)S(1)} %broadcast_dynamic-update-slice_fusion.1, f32[6,4,32,256]{3,2,1,0:T(8,128)} %param.6, f32[4]{0:T(128)S(1)} %get-tuple-element.26, s32[4,32,256]{2,1,0:T(8,128)} %param.7), kind=kLoop, calls=%fused_computation.110 | loop fusion | flops 622592 | bytes 1049088
  1.5 1.1 fusion.13
  2.5 3.2 %collective-permute-start.5 = (f32[7,4,32,3]{3,2,1,0:T(8,128)}, f32[7,4,32,3]{3,2,1,0:T(8,128)}, u32[]{:S(2)}, u32[]{:S(2)}) collective-permute-start(f32[7,4,32,3]{3,2,1,0:T(8,128)} %get-tuple-element.20), channel_id=1, source_target_pairs={{8,0},{16,8},{24,16},{0,24},{9,1},{17,9},{25,17},{1,25},{10,2},{18... | collective-permute-start | bytes 32264 | tf_op jit(solution)/shard_map/ppermute | solution.py:45
  5.7 1.2 %fusion.11 = (f32[7,3,32,256]{3,2,1,0:T(8,128)}, f32[7,3,32,256]{3,2,1,0:T(8,128)}) fusion(f32[6,4,32,256]{3,2,1,0:T(8,128)S(1)} %copy-done, f32[1,4,32,256]{3,2,1,0:T(8,128)S(1)} %bitcast.48), kind=kLoop, calls=%fused_computation.48 | loop fusion | flops 344064 | bytes 2293760 | tf_op jit(solution)/shard_map/concatenate | solution.py:188
  7.0 3.5 %collective-permute-start.2 = (f32[7,3,32,256]{3,2,1,0:T(8,128)}, f32[7,3,32,256]{3,2,1,0:T(8,128)S(1)}, u32[]{:S(2)}, u32[]{:S(2)}) collective-permute-start(f32[7,3,32,256]{3,2,1,0:T(8,128)} %get-tuple-element.22), channel_id=1, source_target_pairs={{32,0},{64,32},{96,64},{128,96},{160,128},{192,160},{224,192},{0,2... | collective-permute-start | bytes 2064392 | tf_op jit(solution)/shard_map/ppermute | solution.py:45
  10.5 0.7 collective-permute-start.4
  11.2 0.7 fusion.48
  11.9 5.6 %collective-permute-start.6 = (f32[7,4,3,256]{3,2,1,0:T(4,128)}, f32[7,4,3,256]{3,2,1,0:T(4,128)}, u32[]{:S(2)}, u32[]{:S(2)}) collective-permute-start(f32[7,4,3,256]{3,2,1,0:T(4,128)} %get-tuple-element.18), channel_id=1, source_target_pairs={{1,0},{2,1},{3,2},{4,3},{5,4},{6,5},{7,6},{0,7},{9,8},{10,9},{11,1... | collective-permute-start | bytes 258056 | tf_op jit(solution)/shard_map/ppermute | solution.py:45
  17.6 0.6 fusion.50
  18.2 0.7 fusion.21
  19.0 1.1 %pad.16 = f32[7,10,32,3]{3,2,1,0:T(8,128)S(1)} pad(f32[7,4,32,3]{3,2,1,0:T(8,128)} %collective-permute-done.5, f32[]{:T(128)} %constant.39.clone.1), padding=0_0x3_3x0_0x0_0 | pad | bytes 37636 | tf_op jit(solution)/shard_map/jit(_pad)/pad | solution.py:51
  20.1 26.0 %collective-permute-done.4 = f32[7,4,32,3]{3,2,1,0:T(8,128)} collective-permute-done((f32[7,4,32,3]{3,2,1,0:T(8,128)}, f32[7,4,32,3]{3,2,1,0:T(8,128)}, u32[]{:S(2)}, u32[]{:S(2)}) %collective-permute-start.4) | collective-permute-done | bytes 10784 | tf_op jit(solution)/shard_map/ppermute | solution.py:44
  46.1 1.2 %pad.15 = f32[7,10,32,3]{3,2,1,0:T(8,128)S(1)} pad(f32[7,4,32,3]{3,2,1,0:T(8,128)} %collective-permute-done.4, f32[]{:T(128)} %constant.39.clone.1), padding=0_0x3_3x0_0x0_0 | pad | bytes 37636 | tf_op jit(solution)/shard_map/jit(_pad)/pad | solution.py:51
  47.3 6.7 %select_maximum_fusion = f32[7,10,38,262]{3,2,1,0:T(8,128)S(1)} fusion(f32[7,4,3,256]{3,2,1,0:T(4,128)} %collective-permute-done.6, f32[7,4,3,256]{3,2,1,0:T(4,128)} %collective-permute-done.3, f32[7,10,32,3]{3,2,1,0:T(8,128)S(1)} %pad.16, f32[7,3,32,256]{3,2,1,0:T(8,128)S(1)} %collective-permute-done.2, f32[1,4,32,256]{3,2,1,0:T(8,128)S(1)} %bitcast.51, ...), kind=kLoop, calls=%fused_computation | loop fusion | flops 7666120 | bytes 5307232 | tf_op jit(solution)/shard_map/concatenate | solution.py:51
  54.9 0.3 fusion.28
  55.2 0.3 fusion.27
  55.5 0.3 fusion.25
  55.7 0.3 fusion.24
  56.4 0.5 add_multiply_fusion.1
  56.9 0.4 copy-done.1
  57.7 0.4 add_multiply_fusion.2
  58.1 4.1 %collective-permute-done = f32[7,3,32,256]{3,2,1,0:T(8,128)S(1)} collective-permute-done((f32[7,3,32,256]{3,2,1,0:T(8,128)}, f32[7,3,32,256]{3,2,1,0:T(8,128)S(1)}, u32[]{:S(2)}, u32[]{:S(2)}) %collective-permute-start) | collective-permute-done | bytes 688160 | tf_op jit(solution)/shard_map/ppermute | solution.py:33
  62.9 0.9 add_multiply_fusion
  63.8 5.9 %divide_add_fusion = f32[6,4,32,257]{3,2,1,0:T(8,128)S(1)} fusion(f32[6,4,32,262]{3,2,1,0:T(8,128)S(1)} %subtract_multiply_fusion.1, f32[6,4,32,262]{3,2,1,0:T(8,128)S(1)} %get-tuple-element.11), kind=kLoop, calls=%fused_computation.21 | loop fusion | flops 25461504 | bytes 8684544 | tf_op jit(solution)/shard_map/add | solution.py:120
  69.7 5.0 %divide_add_fusion.1 = f32[6,4,33,256]{3,2,1,0:T(8,128)S(1)} fusion(f32[6,4,38,256]{3,2,1,0:T(8,128)S(1)} %get-tuple-element.14, f32[6,4,38,256]{3,2,1,0:T(8,128)S(1)} %get-tuple-element.13), kind=kLoop, calls=%fused_computation.25 | loop fusion | flops 26155008 | bytes 8921088 | tf_op jit(solution)/shard_map/add | solution.py:120
  74.8 4.7 %add_multiply_fusion.3 = f32[6,5,32,256]{3,2,1,0:T(8,128)S(1)} fusion(f32[6,10,32,256]{3,2,1,0:T(8,128)S(1)} %get-tuple-element.16, f32[6,10,32,256]{3,2,1,0:T(8,128)S(1)} %get-tuple-element.15, f32[5]{0:T(128)S(1)} %add_convert_fusion), kind=kLoop, calls=%fused_computation.28 | loop fusion | flops 31948800 | bytes 10813460 | tf_op jit(solution)/shard_map/mul | solution.py:131
  79.5 0.7 fusion.6
  80.2 0.9 fusion.51
  81.0 1.4 %broadcast_in_dim.54 = f32[4,6,4,32,128]{4,3,2,1,0:T(8,128)} broadcast(f32[6,4,32,128]{3,2,1,0:T(8,128)S(1)} %fusion.51), dimensions={1,2,3,4} | broadcast | bytes 1966080 | tf_op jit(solution)/shard_map/broadcast_in_dim | solution.py:21
  82.4 5.6 %all-to-all-start = ((f32[4,6,4,32,128]{4,3,2,1,0:T(8,128)}), f32[4,6,4,32,128]{4,3,2,1,0:T(8,128)S(1)}, u32[]{:S(2)}, u32[]{:S(2)}) async-start(f32[4,6,4,32,128]{4,3,2,1,0:T(8,128)} %broadcast_in_dim.54), calls=%async_computation | async-start | bytes 3145728 | tf_op jit(solution)/shard_map/all_to_all | solution.py:22
  88.2 18.9 %all-to-all-done = f32[4,6,4,32,128]{4,3,2,1,0:T(8,128)S(1)} async-done(((f32[4,6,4,32,128]{4,3,2,1,0:T(8,128)}), f32[4,6,4,32,128]{4,3,2,1,0:T(8,128)S(1)}, u32[]{:S(2)}, u32[]{:S(2)}) %all-to-all-start) | async-done | bytes 1572896 | tf_op jit(solution)/shard_map/all_to_all | solution.py:22
  107.3 1.7 %convolution_select_fusion = f32[6,4,32,256]{3,2,1,0:T(8,128)} fusion(f32[6,4,32,256]{3,2,1,0:T(8,128)S(1)} %fusion.6, f32[6,4,32,128]{3,2,1,0:T(8,128)S(1)} %reduce_sum.9, pred[]{:T(512)S(6)} %eq.25, f32[4,128]{1,0:T(4,128)S(1)} %pad_maximum_fusion.10, f32[256,64]{1,0:T(8,128)S(1)} %get-tuple-element.24, f32[256,64]{1,0:T(8,128)S(1)} %get-tuple-element.23), kind=kOutput, calls=%fused_computation.14 | convolution fusion | flops 302317568 | bytes 2099201 | tf_op jit(solution)/shard_map/vizk,tk->vizt/dot_general | solution.py:177
  (47 shorter events, 2.7 us)
Async XLA Ops:
  0.0 1.5 %copy-start = (f32[6,4,32,256]{3,2,1,0:T(8,128)S(1)}, f32[6,4,32,256]{3,2,1,0:T(8,128)}, u32[]{:S(2)}) copy-start(f32[6,4,32,256]{3,2,1,0:T(8,128)} %param.6) | copy-start | bytes 2359300
  2.5 16.4 %collective-permute-start.5 = (f32[7,4,32,3]{3,2,1,0:T(8,128)}, f32[7,4,32,3]{3,2,1,0:T(8,128)}, u32[]{:S(2)}, u32[]{:S(2)}) collective-permute-start(f32[7,4,32,3]{3,2,1,0:T(8,128)} %get-tuple-element.20), channel_id=1, source_target_pairs={{8,0},{16,8},{24,16},{0,24},{9,1},{17,9},{25,17},{1,25},{10,2},{18... | collective-permute-start | bytes 32264 | tf_op jit(solution)/shard_map/ppermute | solution.py:45
  7.0 40.3 %collective-permute-start.2 = (f32[7,3,32,256]{3,2,1,0:T(8,128)}, f32[7,3,32,256]{3,2,1,0:T(8,128)S(1)}, u32[]{:S(2)}, u32[]{:S(2)}) collective-permute-start(f32[7,3,32,256]{3,2,1,0:T(8,128)} %get-tuple-element.22), channel_id=1, source_target_pairs={{32,0},{64,32},{96,64},{128,96},{160,128},{192,160},{224,192},{0,2... | collective-permute-start | bytes 2064392 | tf_op jit(solution)/shard_map/ppermute | solution.py:45
  10.5 36.8 %collective-permute-start.1 = (f32[7,3,32,256]{3,2,1,0:T(8,128)}, f32[7,3,32,256]{3,2,1,0:T(8,128)S(1)}, u32[]{:S(2)}, u32[]{:S(2)}) collective-permute-start(f32[7,3,32,256]{3,2,1,0:T(8,128)} %get-tuple-element.21), channel_id=1, source_target_pairs={{0,32},{32,64},{64,96},{96,128},{128,160},{160,192},{192,224},{224... | collective-permute-start | bytes 2064392 | tf_op jit(solution)/shard_map/ppermute | solution.py:44
  10.5 35.6 %collective-permute-start.4 = (f32[7,4,32,3]{3,2,1,0:T(8,128)}, f32[7,4,32,3]{3,2,1,0:T(8,128)}, u32[]{:S(2)}, u32[]{:S(2)}) collective-permute-start(f32[7,4,32,3]{3,2,1,0:T(8,128)} %get-tuple-element.19), channel_id=1, source_target_pairs={{0,8},{8,16},{16,24},{24,0},{1,9},{9,17},{17,25},{25,1},{2,10},{10... | collective-permute-start | bytes 32264 | tf_op jit(solution)/shard_map/ppermute | solution.py:44
  11.9 35.3 %collective-permute-start.6 = (f32[7,4,3,256]{3,2,1,0:T(4,128)}, f32[7,4,3,256]{3,2,1,0:T(4,128)}, u32[]{:S(2)}, u32[]{:S(2)}) collective-permute-start(f32[7,4,3,256]{3,2,1,0:T(4,128)} %get-tuple-element.18), channel_id=1, source_target_pairs={{1,0},{2,1},{3,2},{4,3},{5,4},{6,5},{7,6},{0,7},{9,8},{10,9},{11,1... | collective-permute-start | bytes 258056 | tf_op jit(solution)/shard_map/ppermute | solution.py:45
  19.0 28.3 %collective-permute-start.3 = (f32[7,4,3,256]{3,2,1,0:T(4,128)S(1)}, f32[7,4,3,256]{3,2,1,0:T(4,128)}, u32[]{:S(2)}, u32[]{:S(2)}) collective-permute-start(f32[7,4,3,256]{3,2,1,0:T(4,128)S(1)} %get-tuple-element.17), channel_id=1, source_target_pairs={{0,1},{1,2},{2,3},{3,4},{4,5},{5,6},{6,7},{7,0},{8,9},{9,10},{10,1... | collective-permute-start | bytes 258056 | tf_op jit(solution)/shard_map/ppermute | solution.py:44
  46.1 16.1 %collective-permute-start = (f32[7,3,32,256]{3,2,1,0:T(8,128)}, f32[7,3,32,256]{3,2,1,0:T(8,128)S(1)}, u32[]{:S(2)}, u32[]{:S(2)}) collective-permute-start(f32[7,3,32,256]{3,2,1,0:T(8,128)} %get-tuple-element.22), channel_id=1, source_target_pairs={{0,16},{8,24},{16,0},{24,8},{1,17},{9,25},{17,1},{25,9},{2,18},{10... | collective-permute-start | bytes 2064392 | tf_op jit(solution)/shard_map/ppermute | solution.py:33
  56.4 0.9 copy-start.1
  57.7 4.5 %copy-start.3 = (f32[7]{0:T(128)S(1)}, f32[7]{0:T(128)}, u32[]{:S(2)}) copy-start(f32[7]{0:T(128)} %constant.69.clone) | copy-start | bytes 88
  74.8 4.7 %copy-start.2 = (f32[6,4,32,256]{3,2,1,0:T(8,128)S(1)}, f32[6,4,32,256]{3,2,1,0:T(8,128)}, u32[]{:S(2)}) copy-start(f32[6,4,32,256]{3,2,1,0:T(8,128)} %param.5) | copy-start | bytes 2359300
  82.4 5.6 %copy-start.4 = (s32[4]{0:T(128)S(1)}, s32[4]{0:T(128)}, u32[]{:S(2)}) copy-start(s32[4]{0:T(128)} %param.8) | copy-start | bytes 52
  82.4 24.7 %all-to-all-start = ((f32[4,6,4,32,128]{4,3,2,1,0:T(8,128)}), f32[4,6,4,32,128]{4,3,2,1,0:T(8,128)S(1)}, u32[]{:S(2)}, u32[]{:S(2)}) async-start(f32[4,6,4,32,128]{4,3,2,1,0:T(8,128)} %broadcast_in_dim.54), calls=%async_computation | async-start | bytes 3145728 | tf_op jit(solution)/shard_map/all_to_all | solution.py:22
where the time goes:
time: 109 us
  waiting for transfers between devices  49 us (45%)
  other arithmetic  34.2 us (31%)
  starting transfers between devices  18.6 us (17%)
  local copies, waits for them, and re-layouts  4.16 us (4%)
  matrix products  2.61 us (2%)
    ppermute x3, waiting for transfers between devices, padded_2(): lax.ppermute(last, axis, up)  26 us
    all_to_all x1, waiting for transfers between devices, from_everyone(): return lax.all_to_all(copies, axis, split_axis=0, concat_axis=0, tiled=True)  18.9 us
    ppermute x3, starting transfers between devices, padded_2(): lax.ppermute(first, axis, [(b, a) for a, b in up])  12.3 us
    add x2, other arithmetic, face_fluxes(): return upwind_part + downwind_part  10.9 us
    concatenate x1, other arithmetic, padded_2(): jnp.concatenate([jnp.pad(low, around), x, jnp.pad(high, around)], axis=dim)  6.69 us
    all_to_all x1, starting transfers between devices, from_everyone(): return lax.all_to_all(copies, axis, split_axis=0, concat_axis=0, tiled=True)  5.59 us
    mul x1, other arithmetic, tendency(): weighted = face_radius * radial_flux  4.7 us
    ppermute x1, waiting for transfers between devices, passed_along(): return lax.ppermute(value, axis, pairs)  4.15 us
  transfers between devices with their start and end apart: 8, of which 3 were waited for; matrix products, arithmetic and copies ran while one was open for 15% of the time, Pallas kernels for 0%

commit v1 on v0

v1 whole, which is shorter than its diff:
```python
import math

import jax
import jax.numpy as jnp
from jax import lax
from jax.experimental import pallas as pl
from jax.experimental.pallas import tpu as pltpu
from jax.sharding import PartitionSpec as P


NT = 1024
KMODES = 64
LANES = 128
SUB = 8

split_speed = 10.0
time_step = 0.05
weno_epsilon = 1e-06
liquid_ratio = 4.4
gas_ratio = 1.4
liquid_stiffness = 0.6
f32 = jnp.float32


def pressure_at(q, phase):
    kinetic = 0.5 * (q[1] * q[1] + q[2] * q[2] + q[3] * q[3]) / q[0]
    liquid = phase == 1
    heat_ratio = jnp.where(liquid, liquid_ratio, gas_ratio)
    stiffness = jnp.where(liquid, liquid_stiffness, 0.0)
    return (heat_ratio - 1.0) * (q[4] - kinetic) - heat_ratio * stiffness


def doubled_fluxes(q, channel, component, velocity):
    physical = q[channel] * velocity
    if channel == component:
        physical = physical + q[6]
    if channel == 4:
        physical = (q[4] + q[6]) * velocity
    carried = split_speed * q[channel]
    return physical + carried, physical - carried


def curvature(before, centre, after):
    step_low = centre - before
    step_high = after - centre
    second = step_high - step_low
    half = 0.5 * second
    base = (13.0 / 12.0) * (second * second) + 4.0 * weno_epsilon
    left = step_high + half
    mid = step_low + half
    right = step_low - half
    return left * left + base, mid * mid + base, right * right + base, second


def weighted_shift(beta_0, beta_1, beta_2, third_0, third_2):
    p = beta_1 * beta_2
    r = beta_0 * beta_2
    s = beta_0 * beta_1
    c_0 = p * p
    c_1 = 6.0 * (r * r)
    c_2 = 3.0 * (s * s)
    return ((c_0 + c_0) * third_0 + c_2 * third_2) / (c_0 + c_1 + c_2)


def centred(near, centre, far):
    return 5.0 * centre - near + 2.0 * far


SEG = 32
EXT = SEG + 2 * SUB
ROWS = EXT + SUB


def sweep(load, component, emit, scratch):
    up_ref, down_ref, face_ref = scratch[0], scratch[1], scratch[2]
    lists = scratch[3:]
    blocks = EXT // SUB
    cells = [[load(c, b) for c in range(7)] for b in range(blocks)]
    speed = [q[component] / q[0] for q in cells]
    for c in range(6):
        for b in range(blocks):
            up, down = doubled_fluxes(cells[b], c, component, speed[b])
            up_ref[c, b * SUB : (b + 1) * SUB, :] = up
            down_ref[c, b * SUB : (b + 1) * SUB, :] = down
    for c in range(6):
        for side, ref in ((0, up_ref), (1, down_ref)):
            for b in range(5):
                row = 6 + b * SUB
                vals = curvature(
                    ref[c, row - 1 : row - 1 + SUB, :],
                    ref[c, row : row + SUB, :],
                    ref[c, row + 1 : row + 1 + SUB, :],
                )
                for k in range(4):
                    lists[side * 4 + k][c, row : row + SUB, :] = vals[k]
    for c in range(6):
        for b in range(5):
            j = SUB + b * SUB

            def at(ref, off):
                return ref[c, j + off : j + off + SUB, :]

            la, ca, ra, sa = lists[0:4]
            s0, s1, s2 = at(sa, -2), at(sa, -1), at(sa, 0)
            up_part = weighted_shift(at(la, -2), at(ca, -1), at(ra, 0), s0 - s1, s1 - s2)
            lb, cb, rb, sb = lists[4:8]
            s0, s1, s2 = at(sb, 1), at(sb, 0), at(sb, -1)
            down_part = weighted_shift(at(rb, 1), at(cb, 0), at(lb, -1), s0 - s1, s1 - s2)
            total = up_part + down_part
            total = total + centred(at(up_ref, -2), at(up_ref, -1), at(up_ref, 0))
            total = total + centred(at(down_ref, 1), at(down_ref, 0), at(down_ref, -1))
            face_ref[c, b * SUB : (b + 1) * SUB, :] = total
        for b in range(SEG // SUB):
            low = face_ref[c, b * SUB : (b + 1) * SUB, :]
            high = face_ref[c, b * SUB + 1 : b * SUB + 1 + SUB, :]
            emit(c, b, high - low)


def sweep_scratch():
    return [pltpu.VMEM((6, ROWS, LANES), f32) for _ in range(11)]


def pack_body(section_ref, phase_ref, bottom_ref, top_ref, pressure_ref, first_ref, last_ref):
    cycles, depth = section_ref.shape[1], section_ref.shape[2]
    for k in range(cycles):
        q = [section_ref[c, k] for c in range(6)]
        q.append(pressure_at(q, phase_ref[k]))
        pressure_ref[k] = q[6]
        for c in range(7):
            if k < 3:
                bottom_ref[c, k] = q[c]
            if k > 0:
                top_ref[c, k - 1] = q[c]
            first_ref[c * cycles + k] = q[c][:SUB]
            last_ref[c * cycles + k] = q[c][depth - SUB :]


def pack_call(section, phase):
    _, cycles, depth, width = section.shape
    layers = jax.ShapeDtypeStruct((7, 3, depth, width), f32)
    edge = jax.ShapeDtypeStruct((7 * cycles, SUB, width), f32)
    pressure = jax.ShapeDtypeStruct((cycles, depth, width), f32)
    return pl.pallas_call(pack_body, out_shape=(layers, layers, pressure, edge, edge), name="pack")(
        section, phase
    )


def turn_body(section_ref, pressure_ref, turned_ref, first_ref, last_ref):
    cycles, depth, width = pressure_ref.shape
    for c in range(7):
        q = section_ref[c] if c < 6 else pressure_ref[...]
        q = q.reshape(cycles * depth, width)
        for h in range(width // LANES):
            t = q[:, h * LANES : (h + 1) * LANES].T
            turned_ref[c, h * LANES : (h + 1) * LANES, :] = t
            if h == 0:
                first_ref[c] = t[:SUB]
            if h == width // LANES - 1:
                last_ref[c] = t[LANES - SUB :]


def turn_call(section, pressure):
    cycles, depth, width = pressure.shape
    turned = jax.ShapeDtypeStruct((7, width, cycles * depth), f32)
    edge = jax.ShapeDtypeStruct((7, SUB, cycles * depth), f32)
    return pl.pallas_call(turn_body, out_shape=(turned, edge, edge), name="turn")(section, pressure)


def axial_body(start_ref, section_ref, pressure_ref, before_ref, after_ref, out_ref, *scratch):
    cycles, _, width = pressure_ref.shape
    first = lax.axis_index("row") * cycles

    @pl.loop(0, cycles)
    def _(k):
        radius = (first + k).astype(f32) + 0.5
        for h in range(width // LANES):
            lanes = slice(h * LANES, (h + 1) * LANES)

            def load(c, b):
                if b == 0:
                    return before_ref[c * cycles + k, :, lanes]
                if b == EXT // SUB - 1:
                    return after_ref[c * cycles + k, :, lanes]
                rows = slice((b - 1) * SUB, b * SUB)
                return section_ref[c, k, rows, lanes] if c < 6 else pressure_ref[k, rows, lanes]

            def emit(c, b, change):
                rows = slice(b * SUB, (b + 1) * SUB)
                value = 0.25 * section_ref[c, k, rows, lanes] - (0.25 * time_step / 12.0) * change
                if c in (1, 2):
                    swirl = section_ref[2, k, rows, lanes] / section_ref[0, k, rows, lanes]
                    if c == 1:
                        source = section_ref[2, k, rows, lanes] * swirl + pressure_ref[k, rows, lanes]
                    else:
                        source = -section_ref[1, k, rows, lanes] * swirl
                    value = value + (0.25 * time_step) * (source / radius)
                out_ref[c, k, rows, lanes] = 0.75 * start_ref[c, k, rows, lanes] + value

            sweep(load, 3, emit, scratch)


def axial_call(start, section, pressure, before, after):
    return pl.pallas_call(
        axial_body,
        out_shape=jax.ShapeDtypeStruct(section.shape, f32),
        scratch_shapes=sweep_scratch(),
        name="axial",
    )(start, section, pressure, before, after)


def swirl_body(partial_ref, turned_ref, before_ref, after_ref, out_ref, ext_ref, div_ref, *scratch):
    width = turned_ref.shape[1]
    cycles, depth = partial_ref.shape[1], partial_ref.shape[2]
    first = lax.axis_index("row") * cycles
    for c in range(7):
        ext_ref[c, 0:SUB, :] = before_ref[c]
        ext_ref[c, SUB + width : 2 * SUB + width, :] = after_ref[c]
        ext_ref[c, SUB : SUB + width, :] = turned_ref[c]

    @pl.loop(0, width // SEG)
    def _(n):
        origin = pl.multiple_of(n * SEG, SEG)

        def load(c, b):
            return ext_ref[c, pl.ds(origin + b * SUB, SUB), :]

        def emit(c, b, change):
            div_ref[c, pl.ds(origin + b * SUB, SUB), :] = change

        sweep(load, 2, emit, scratch)

    angle_step = 2.0 * math.pi / NT
    for c in range(6):
        for h in range(width // LANES):
            lanes = slice(h * LANES, (h + 1) * LANES)
            div = div_ref[c, h * LANES : (h + 1) * LANES, :].T
            div = div.reshape(cycles, depth, LANES)
            for k in range(cycles):
                radius = (first + k).astype(f32) + 0.5
                scale = (0.25 * time_step / 12.0) / (radius * angle_step)
                out_ref[c, k, :, lanes] = partial_ref[c, k, :, lanes] - scale * div[k]


def swirl_call(partial, turned, before, after):
    width = turned.shape[1]
    return pl.pallas_call(
        swirl_body,
        out_shape=jax.ShapeDtypeStruct(partial.shape, f32),
        scratch_shapes=[
            pltpu.VMEM((7, width + 2 * SUB, LANES), f32),
            pltpu.VMEM((6, width, LANES), f32),
        ]
        + sweep_scratch(),
        name="swirl",
    )(partial, turned, before, after)


def radial_parts(load, cell_list):
    cells = {k: [load(c, k) for c in range(7)] for k in cell_list}
    speed = {k: q[1] / q[0] for k, q in cells.items()}
    for c in range(6):
        pairs = {k: doubled_fluxes(cells[k], c, 1, speed[k]) for k in cell_list}
        yield c, {k: v[0] for k, v in pairs.items()}, {k: v[1] for k, v in pairs.items()}


def face_up(y, j, curves):
    s0, s1, s2 = curves[j - 2][3], curves[j - 1][3], curves[j][3]
    shift = weighted_shift(curves[j - 2][0], curves[j - 1][1], curves[j][2], s0 - s1, s1 - s2)
    return shift + centred(y[j - 2], y[j - 1], y[j])


def face_down(y, j, curves):
    s0, s1, s2 = curves[j + 1][3], curves[j][3], curves[j - 1][3]
    shift = weighted_shift(curves[j + 1][2], curves[j][1], curves[j - 1][0], s0 - s1, s1 - s2)
    return shift + centred(y[j + 1], y[j], y[j - 1])


def curves_of(y, cells):
    return {m: curvature(y[m - 1], y[m], y[m + 1]) for m in cells}


def scales_of(cycles, first):
    edge = [(first + k).astype(f32) for k in range(cycles + 1)]
    scale = [(0.25 * time_step / 12.0) / (edge[k] + 0.5) for k in range(cycles)]
    return edge, scale


def outer_body(partial_ref, section_ref, pressure_ref, halo_ref, out_ref):
    cycles = section_ref.shape[1]
    row = lax.axis_index("row")
    last = row == lax.axis_size("row") - 1
    edge, scale = scales_of(cycles, row * cycles)
    for h in range(section_ref.shape[3] // LANES):
        lanes = slice(h * LANES, (h + 1) * LANES)

        def load(c, k):
            own = min(k, cycles - 1)
            mine = section_ref[c, own, :, lanes] if c < 6 else pressure_ref[own, :, lanes]
            if k < cycles:
                return mine
            return jnp.where(last, mine, halo_ref[c, k - cycles, :, lanes])

        for c, up, down in radial_parts(load, range(7)):
            cu = curves_of(up, (1, 2, 3, 4))
            cd = curves_of(down, (1, 2, 3, 4, 5))
            half_2 = edge[2] * face_down(down, 2, cd)
            face_3 = edge[3] * (face_up(up, 3, cu) + face_down(down, 3, cd))
            face_4 = edge[4] * (face_up(up, 4, cu) + face_down(down, 4, cd))
            out_ref[c, 0, :, lanes] = partial_ref[c, 0, :, lanes]
            out_ref[c, 1, :, lanes] = partial_ref[c, 1, :, lanes] - scale[1] * half_2
            out_ref[c, 2, :, lanes] = partial_ref[c, 2, :, lanes] - scale[2] * (face_3 - half_2)
            out_ref[c, 3, :, lanes] = partial_ref[c, 3, :, lanes] - scale[3] * (face_4 - face_3)


def inner_body(partial_ref, section_ref, pressure_ref, halo_ref, mirror_ref, out_ref):
    cycles = section_ref.shape[1]
    row = lax.axis_index("row")
    axis = row == 0
    edge, scale = scales_of(cycles, row * cycles)
    for h in range(section_ref.shape[3] // LANES):
        lanes = slice(h * LANES, (h + 1) * LANES)

        def load(c, k):
            if k >= 0:
                return section_ref[c, k, :, lanes] if c < 6 else pressure_ref[k, :, lanes]
            across = mirror_ref[c, -1 - k, :, lanes]
            if c in (1, 2):
                across = -across
            return jnp.where(axis, across, halo_ref[c, 3 + k, :, lanes])

        for c, up, down in radial_parts(load, range(-3, 4)):
            cu = curves_of(up, (-2, -1, 0, 1, 2))
            cd = curves_of(down, (-1, 0, 1, 2))
            face_0 = edge[0] * (face_up(up, 0, cu) + face_down(down, 0, cd))
            face_1 = edge[1] * (face_up(up, 1, cu) + face_down(down, 1, cd))
            half_2 = edge[2] * face_up(up, 2, cu)
            out_ref[c, 0, :, lanes] = partial_ref[c, 0, :, lanes] - scale[0] * (face_1 - face_0)
            out_ref[c, 1, :, lanes] = partial_ref[c, 1, :, lanes] - scale[1] * (half_2 - face_1)
            out_ref[c, 2, :, lanes] = partial_ref[c, 2, :, lanes] + scale[2] * half_2
            out_ref[c, 3, :, lanes] = partial_ref[c, 3, :, lanes]


def radial_call(body, partial, section, pressure, *halos):
    channels, cycles, depth, width = section.shape
    state = pl.BlockSpec((channels, cycles, SUB, width), lambda i: (0, 0, i, 0))
    halo = pl.BlockSpec((7, 3, SUB, width), lambda i: (0, 0, i, 0))
    return pl.pallas_call(
        body,
        out_shape=jax.ShapeDtypeStruct(partial.shape, f32),
        grid=(depth // SUB,),
        in_specs=[state, state, pl.BlockSpec((cycles, SUB, width), lambda i: (0, i, 0))]
        + [halo] * len(halos),
        out_specs=state,
    )(partial, section, pressure, *halos)


def build_table(positions, mode_count, length):
    orders = lax.iota(jnp.int32, mode_count)
    phases = positions[:, None] * orders[None, :] % length
    angles = phases.astype(jnp.float32) * (2.0 * math.pi / length)
    return jnp.concatenate([jnp.cos(angles), jnp.sin(angles)], 1)


def cycle_weights(cutoff, mode_count, length):
    orders = lax.iota(jnp.int32, mode_count)
    mode_scale = jnp.where(orders == 0, 1.0 / length, 2.0 / length)
    kept_modes = orders[None, :] <= cutoff[:, None]
    weight_half = jnp.where(kept_modes, mode_scale[None, :], 0.0)
    return jnp.concatenate([weight_half, weight_half], 1)


def sum_over_theta(coefficients, theta_id):
    half = coefficients.shape[2] // 2
    core = theta_id % 2
    core_swap = [(0, 1), (1, 0), (2, 3), (3, 2)]
    chip_swap = [(0, 2), (2, 0), (1, 3), (3, 1)]
    axes = ("row", "theta")
    low, high = coefficients[:, :, :half], coefficients[:, :, half:]
    mine = jnp.where(core == 0, low, high)
    other = jnp.where(core == 0, high, low)
    mine = mine + lax.ppermute(other, axes, core_swap)
    mine = mine + lax.ppermute(mine, axes, chip_swap)
    other = lax.ppermute(mine, axes, core_swap)
    low = jnp.where(core == 0, mine, other)
    high = jnp.where(core == 0, other, mine)
    return jnp.concatenate([low, high], 2)


def ring(count):
    up = [(i, (i + 1) % count) for i in range(count)]
    return up, [(b, a) for a, b in up]


def shards(state_start, state_section, phase, cutoff):
    row_count = lax.axis_size("row")
    row_id = lax.axis_index("row")
    theta_count = lax.axis_size("theta")
    theta_id = lax.axis_index("theta")
    gz_count = lax.axis_size("gz")

    bottom, top, pressure, z_first, z_last = pack_call(state_section, phase)
    across = [(t, (t + theta_count // 2) % theta_count) for t in range(theta_count)]
    mirror = lax.ppermute(bottom, ("row", "theta"), across)
    above = lax.ppermute(bottom, "row", [(r + 1, r) for r in range(row_count - 1)])
    turned, t_first, t_last = turn_call(state_section, pressure)
    up, down = ring(theta_count)
    t_before = lax.ppermute(t_last, "theta", up)
    t_after = lax.ppermute(t_first, "theta", down)
    below = lax.ppermute(top, "row", [(r, r + 1) for r in range(row_count - 1)])
    up, down = ring(gz_count)
    z_before = lax.ppermute(z_last, "gz", up)
    z_after = lax.ppermute(z_first, "gz", down)

    partial = axial_call(state_start, state_section, pressure, z_before, z_after)
    partial = swirl_call(partial, turned, t_before, t_after)
    partial = radial_call(outer_body, partial, state_section, pressure, above)
    advanced = radial_call(inner_body, partial, state_section, pressure, below, mirror)

    weights = cycle_weights(cutoff, KMODES, NT)
    local_theta = advanced.shape[3]
    positions = theta_id * local_theta + lax.iota(jnp.int32, local_theta)
    table = build_table(positions, KMODES, NT)
    exact = lax.Precision.HIGHEST
    coefficients = jnp.einsum("vizt,tk->vizk", advanced, table, precision=exact)
    coefficients = sum_over_theta(coefficients, theta_id)
    coefficients = coefficients * weights[None, :, None, :]
    filtered = jnp.einsum("vizk,tk->vizt", coefficients, table, precision=exact)
    return jnp.where(row_id == 0, filtered, advanced)


def solution(mesh):
    in_specs = (
        P(None, "row", "gz", "theta"),
        P(None, "row", "gz", "theta"),
        P("row", "gz", "theta"),
        P(),
    )
    out_specs = P(None, "row", "gz", "theta")
    return jax.shard_map(shards, mesh=mesh, in_specs=in_specs, out_specs=out_specs, check_vma=False)
```

time: 109 us -> 77.4 us (0.71)
  other arithmetic: 34.2 us -> 0.86 us
  waiting for transfers between devices: 49 us -> 17.7 us
  Pallas kernels: 0 us -> 25.8 us
  starting transfers between devices: 18.6 us -> 25.3 us
  matrix products: 2.61 us -> 3.73 us
    pallas_call x0 -> x6, Pallas kernels: none -> 25.8 us  [the longest x2 9.21 us: radial_call(): pl.pallas_call(body, out_shape=jax.ShapeDtypeStruct(partial.shape, f32),...]
    all_to_all x1 -> x0, waiting for transfers between devices: 18.9 us -> none  [from_everyone(): return lax.all_to_all(copies, axis, split_axis=0, concat_axis=0, tiled=True)]
    ppermute x7 -> x10, waiting for transfers between devices: 30.1 us -> 17.7 us  [the longest x1 6.31 us: shards(): t_before = lax.ppermute(t_last, 'theta', up)]
    ppermute x7 -> x10, starting transfers between devices: 13 us -> 25.3 us  [the longest x1 4.03 us: shards(): z_after = lax.ppermute(z_first, 'gz', down)]
    add x4 -> x3, other arithmetic: 11.6 us -> 0.07 us  [the longest x1 0.04 us: sum_over_theta(): mine = mine + lax.ppermute(other, axes, core_swap)]
    concatenate x5 -> x0, other arithmetic: 9.86 us -> none  [the longest x1 6.69 us: padded_2(): jnp.concatenate([jnp.pad(low, around), x, jnp.pad(high, around)], axis=dim)]
    mul x5 -> x0, other arithmetic: 6.67 us -> none  [the longest x1 4.7 us: tendency(): weighted = face_radius * radial_flux]
    all_to_all x1 -> x0, starting transfers between devices: 5.59 us -> none  [from_everyone(): return lax.all_to_all(copies, axis, split_axis=0, concat_axis=0, tiled=True)]
  transfers between devices with their start and end apart: 8 -> 10, of which waited for: 3 -> 6; matrix products, arithmetic and copies ran while one was open for 15% -> 1% of each run, Pallas kernels for 0% -> 24%
where the time goes in v1:
time: 77.4 us; the launch traced here: 76.9 us
  Pallas kernels  25.8 us (33%)
  starting transfers between devices  25.3 us (33%)
  waiting for transfers between devices  17.7 us (23%)
  matrix products  3.73 us (5%)
  local copies, waits for them, and re-layouts  3.27 us (4%)
  other arithmetic  0.86 us (1%)
    pallas_call x2, Pallas kernels, radial_call(): pl.pallas_call(body, out_shape=jax.ShapeDtypeStruct(partial.shape, f32),...  9.21 us
    ppermute x1, waiting for transfers between devices, shards(): t_before = lax.ppermute(t_last, 'theta', up)  6.31 us
    pallas_call x1, Pallas kernels, swirl_call(): pl.pallas_call(swirl_body, out_shape=jax.ShapeDtypeStruct(partial.shape,...  5.84 us
    pallas_call x1, Pallas kernels, axial_call(): pl.pallas_call(axial_body, out_shape=jax.ShapeDtypeStruct(section.shape,...  5.79 us
    ppermute x1, waiting for transfers between devices, sum_over_theta(): mine = mine + lax.ppermute(mine, axes, chip_swap)  4.84 us
    ppermute x1, starting transfers between devices, shards(): z_after = lax.ppermute(z_first, 'gz', down)  4.03 us
    ppermute x1, starting transfers between devices, shards(): mirror = lax.ppermute(bottom, ('row', 'theta'), across)  3.94 us
    ppermute x1, starting transfers between devices, sum_over_theta(): mine = mine + lax.ppermute(mine, axes, chip_swap)  3.49 us
  transfers between devices with their start and end apart: 10, of which 6 were waited for; matrix products, arithmetic and copies ran while one was open for 1% of the time, Pallas kernels for 24%

profile of v1, /device:TPU:1, one launch (start us, length us, event | category | flops | bytes accessed | tf_op | source)
XLA Modules:
  0.0 76.9 jit_solution(17341484568245808690)
XLA Ops:
  0.0 2.5 %pack.1 = (f32[7,3,32,256]{3,2,1,0:T(8,128)}, f32[7,3,32,256]{3,2,1,0:T(8,128)}, f32[4,32,256]{2,1,0:T(8,128)}, f32[28,8,256]{2,1,0:T(8,128)}, f32[28,8,256]{2,1,0:T(8,128)}) custom-call(f32[6,4,32,256]{3,2,1,0:T(8,128)} %section_ref.9, s32[4,32,256]{2,1,0:T(8,128)} %phase_ref.1), custom_call_target="tpu_custom_call" | custom-call | tf_op jit(solution)/shard_map/pack/pallas_call | solution.py:143
  2.5 1.3 %collective-permute-start.4 = (f32[7,3,32,256]{3,2,1,0:T(8,128)}, f32[7,3,32,256]{3,2,1,0:T(8,128)S(1)}, u32[]{:S(2)}, u32[]{:S(2)}) collective-permute-start(f32[7,3,32,256]{3,2,1,0:T(8,128)} %get-tuple-element.19), channel_id=1, source_target_pairs={{32,0},{64,32},{96,64},{128,96},{160,128},{192,160},{224,192},{33,... | collective-permute-start | bytes 2064392 | tf_op jit(solution)/shard_map/ppermute | solution.py:404
  3.8 3.9 %collective-permute-start.6 = (f32[7,3,32,256]{3,2,1,0:T(8,128)}, f32[7,3,32,256]{3,2,1,0:T(8,128)S(1)}, u32[]{:S(2)}, u32[]{:S(2)}) collective-permute-start(f32[7,3,32,256]{3,2,1,0:T(8,128)} %get-tuple-element.19), channel_id=1, source_target_pairs={{0,16},{8,24},{16,0},{24,8},{1,17},{9,25},{17,1},{25,9},{2,18},{10... | collective-permute-start | bytes 2064392 | tf_op jit(solution)/shard_map/ppermute | solution.py:403
  7.8 2.9 %collective-permute-start.5 = (f32[7,3,32,256]{3,2,1,0:T(8,128)}, f32[7,3,32,256]{3,2,1,0:T(8,128)S(1)}, u32[]{:S(2)}, u32[]{:S(2)}) collective-permute-start(f32[7,3,32,256]{3,2,1,0:T(8,128)} %get-tuple-element.20), channel_id=1, source_target_pairs={{0,32},{32,64},{64,96},{96,128},{128,160},{160,192},{192,224},{1,3... | collective-permute-start | bytes 2064392 | tf_op jit(solution)/shard_map/ppermute | solution.py:409
  10.7 1.9 %collective-permute-start = (f32[28,8,256]{2,1,0:T(8,128)}, f32[28,8,256]{2,1,0:T(8,128)S(1)}, u32[]{:S(2)}, u32[]{:S(2)}) collective-permute-start(f32[28,8,256]{2,1,0:T(8,128)} %get-tuple-element.14), channel_id=1, source_target_pairs={{0,1},{1,2},{2,3},{3,4},{4,5},{5,6},{6,7},{7,0},{8,9},{9,10},{10,1... | collective-permute-start | bytes 688136 | tf_op jit(solution)/shard_map/ppermute | solution.py:411
  12.6 4.0 %collective-permute-start.1 = (f32[28,8,256]{2,1,0:T(8,128)}, f32[28,8,256]{2,1,0:T(8,128)S(1)}, u32[]{:S(2)}, u32[]{:S(2)}) collective-permute-start(f32[28,8,256]{2,1,0:T(8,128)} %get-tuple-element.15), channel_id=1, source_target_pairs={{1,0},{2,1},{3,2},{4,3},{5,4},{6,5},{7,6},{0,7},{9,8},{10,9},{11,1... | collective-permute-start | bytes 688136 | tf_op jit(solution)/shard_map/ppermute | solution.py:412
  16.6 2.4 %turn.1 = (f32[7,256,128]{2,1,0:T(8,128)}, f32[7,8,128]{2,1,0:T(8,128)}, f32[7,8,128]{2,1,0:T(8,128)}) custom-call(f32[6,4,32,256]{3,2,1,0:T(8,128)} %section_ref.9, f32[4,32,256]{2,1,0:T(8,128)} %get-tuple-element.13.pressure_ref), custom_call_target="tpu_custom_call" | custom-call | tf_op jit(solution)/shard_map/turn/pallas_call | solution.py:166
  19.1 2.5 %collective-permute-done.before_ref = f32[28,8,256]{2,1,0:T(8,128)S(1)} collective-permute-done((f32[28,8,256]{2,1,0:T(8,128)}, f32[28,8,256]{2,1,0:T(8,128)S(1)}, u32[]{:S(2)}, u32[]{:S(2)}) %collective-permute-start) | collective-permute-done | bytes 229408 | tf_op jit(solution)/shard_map/ppermute | solution.py:411
  21.5 2.9 %collective-permute-start.2 = (f32[7,8,128]{2,1,0:T(8,128)}, f32[7,8,128]{2,1,0:T(8,128)S(1)}, u32[]{:S(2)}, u32[]{:S(2)}) collective-permute-start(f32[7,8,128]{2,1,0:T(8,128)} %get-tuple-element.17), channel_id=1, source_target_pairs={{0,8},{8,16},{16,24},{24,0},{1,9},{9,17},{17,25},{25,1},{2,10},{10... | collective-permute-start | bytes 86024 | tf_op jit(solution)/shard_map/ppermute | solution.py:407
  24.4 0.0 collective-permute-done.1.after_ref
  24.4 0.6 fusion.10
  25.1 0.1 copy-done.5
  25.1 5.8 %axial.1.partial_ref = f32[6,4,32,256]{3,2,1,0:T(8,128)} custom-call(f32[6,4,32,256]{3,2,1,0:T(8,128)} %start_ref.1, f32[6,4,32,256]{3,2,1,0:T(8,128)} %section_ref.9, f32[4,32,256]{2,1,0:T(8,128)} %get-tuple-element.13.pressure_ref, f32[28,8,256]{2,1,0:T(8,128)} %copy-done.4, f32[28,8,256]{2,1,0:T(8,128)} %copy-done.5), custom_call_target="tpu_custom_call" | custom-call | tf_op jit(solution)/shard_map/axial/pallas_call | solution.py:203
  30.9 6.3 %collective-permute-done.2.before_ref = f32[7,8,128]{2,1,0:T(8,128)S(1)} collective-permute-done((f32[7,8,128]{2,1,0:T(8,128)}, f32[7,8,128]{2,1,0:T(8,128)S(1)}, u32[]{:S(2)}, u32[]{:S(2)}) %collective-permute-start.2) | collective-permute-done | bytes 28704 | tf_op jit(solution)/shard_map/ppermute | solution.py:407
  37.2 1.8 %collective-permute-done.3.after_ref = f32[7,8,128]{2,1,0:T(8,128)S(1)} collective-permute-done((f32[7,8,128]{2,1,0:T(8,128)}, f32[7,8,128]{2,1,0:T(8,128)S(1)}, u32[]{:S(2)}, u32[]{:S(2)}) %collective-permute-start.3) | collective-permute-done | bytes 28704 | tf_op jit(solution)/shard_map/ppermute | solution.py:408
  39.0 0.6 copy-done.7
  39.6 5.8 %swirl.1.partial_ref = f32[6,4,32,256]{3,2,1,0:T(8,128)} custom-call(f32[6,4,32,256]{3,2,1,0:T(8,128)} %axial.1.partial_ref, f32[7,256,128]{2,1,0:T(8,128)} %get-tuple-element.16.turned_ref, f32[7,8,128]{2,1,0:T(8,128)} %copy-done.6, f32[7,8,128]{2,1,0:T(8,128)} %copy-done.7), custom_call_target="tpu_custom_call" | custom-call | tf_op jit(solution)/shard_map/swirl/pallas_call | solution.py:246
  45.5 0.9 %copy-done.1 = f32[7,3,32,256]{3,2,1,0:T(8,128)} copy-done((f32[7,3,32,256]{3,2,1,0:T(8,128)}, f32[7,3,32,256]{3,2,1,0:T(8,128)S(1)}, u32[]{:S(2)}) %copy-start.1) | copy-done | bytes 688152
  46.4 4.5 %shard_map.46.partial_ref = f32[6,4,32,256]{3,2,1,0:T(8,128)} custom-call(f32[6,4,32,256]{3,2,1,0:T(8,128)} %swirl.1.partial_ref, f32[6,4,32,256]{3,2,1,0:T(8,128)} %section_ref.9, f32[4,32,256]{2,1,0:T(8,128)} %get-tuple-element.13.pressure_ref, f32[7,3,32,256]{3,2,1,0:T(8,128)} %copy-done.1), custom_call_target="tpu_custom_call" | custom-call | tf_op jit(solution)/shard_map/pallas_call | solution.py:347
  50.9 0.9 %copy-done.2 = f32[7,3,32,256]{3,2,1,0:T(8,128)} copy-done((f32[7,3,32,256]{3,2,1,0:T(8,128)}, f32[7,3,32,256]{3,2,1,0:T(8,128)S(1)}, u32[]{:S(2)}) %copy-start.2) | copy-done | bytes 688152
  51.8 0.8 %copy-done.3 = f32[7,3,32,256]{3,2,1,0:T(8,128)} copy-done((f32[7,3,32,256]{3,2,1,0:T(8,128)}, f32[7,3,32,256]{3,2,1,0:T(8,128)S(1)}, u32[]{:S(2)}) %copy-start.3) | copy-done | bytes 688152
  52.6 4.7 %shard_map.47 = f32[6,4,32,256]{3,2,1,0:T(8,128)} custom-call(f32[6,4,32,256]{3,2,1,0:T(8,128)} %shard_map.46.partial_ref, f32[6,4,32,256]{3,2,1,0:T(8,128)} %section_ref.9, f32[4,32,256]{2,1,0:T(8,128)} %get-tuple-element.13.pressure_ref, f32[7,3,32,256]{3,2,1,0:T(8,128)} %copy-done.3, f32[7,3,32,256]{3,2,1,0:T(8,128)} %copy-done.2), custom_call_target="tpu_custom_call" | custom-call | tf_op jit(solution)/shard_map/pallas_call | solution.py:347
  57.3 2.0 %fusion.11 = f32[6,4,32,128]{3,2,1,0:T(8,128)S(1)} fusion(f32[6,4,32,256]{3,2,1,0:T(8,128)} %shard_map.47, f32[256,64]{1,0:T(8,128)S(1)} %get-tuple-element.24, f32[256,64]{1,0:T(8,128)S(1)} %get-tuple-element.23), kind=kOutput, calls=%fused_computation.21 | convolution fusion | flops 302022656 | bytes 1310720 | tf_op jit(solution)/shard_map/vizt,tk->vizk/dot_general | solution.py:424
  59.3 1.9 %collective-permute-start.7 = (f32[6,4,16,128]{3,2,1,0:T(8,128)S(1)}, f32[6,4,16,128]{3,2,1,0:T(8,128)S(1)}, u32[]{:S(2)}, u32[]{:S(2)}) collective-permute-start(f32[6,4,16,128]{3,2,1,0:T(8,128)S(1)} %slice_select_fusion), channel_id=1, source_target_pairs={{0,8},{8,0},{16,24},{24,16},{1,9},{9,1},{17,25},{25,17},{2,10},{10... | collective-permute-start | bytes 589832 | tf_op jit(solution)/shard_map/ppermute | solution.py:381
  61.3 1.4 %collective-permute-done.7 = f32[6,4,16,128]{3,2,1,0:T(8,128)S(1)} collective-permute-done((f32[6,4,16,128]{3,2,1,0:T(8,128)S(1)}, f32[6,4,16,128]{3,2,1,0:T(8,128)S(1)}, u32[]{:S(2)}, u32[]{:S(2)}) %collective-permute-start.7) | collective-permute-done | bytes 196640 | tf_op jit(solution)/shard_map/ppermute | solution.py:381
  62.7 3.5 %collective-permute-start.8 = (f32[6,4,16,128]{3,2,1,0:T(8,128)S(1)}, f32[6,4,16,128]{3,2,1,0:T(8,128)S(1)}, u32[]{:S(2)}, u32[]{:S(2)}) collective-permute-start(f32[6,4,16,128]{3,2,1,0:T(8,128)S(1)} %select_add_fusion), channel_id=1, source_target_pairs={{0,16},{16,0},{8,24},{24,8},{1,17},{17,1},{9,25},{25,9},{2,18},{18... | collective-permute-start | bytes 589832 | tf_op jit(solution)/shard_map/ppermute | solution.py:382
  66.2 4.8 %collective-permute-done.8 = f32[6,4,16,128]{3,2,1,0:T(8,128)S(1)} collective-permute-done((f32[6,4,16,128]{3,2,1,0:T(8,128)S(1)}, f32[6,4,16,128]{3,2,1,0:T(8,128)S(1)}, u32[]{:S(2)}, u32[]{:S(2)}) %collective-permute-start.8) | collective-permute-done | bytes 196640 | tf_op jit(solution)/shard_map/ppermute | solution.py:382
  71.1 2.9 %collective-permute-start.9 = (f32[6,4,16,128]{3,2,1,0:T(8,128)S(1)}, f32[6,4,16,128]{3,2,1,0:T(8,128)S(1)}, u32[]{:S(2)}, u32[]{:S(2)}) collective-permute-start(f32[6,4,16,128]{3,2,1,0:T(8,128)S(1)} %add.31), channel_id=1, source_target_pairs={{0,8},{8,0},{16,24},{24,16},{1,9},{9,1},{17,25},{25,17},{2,10},{10... | collective-permute-start | bytes 589832 | tf_op jit(solution)/shard_map/ppermute | solution.py:383
  74.0 0.1 fusion.12
  74.1 0.1 pad_maximum_fusion
  74.2 0.9 %collective-permute-done.9 = f32[6,4,16,128]{3,2,1,0:T(8,128)S(1)} collective-permute-done((f32[6,4,16,128]{3,2,1,0:T(8,128)S(1)}, f32[6,4,16,128]{3,2,1,0:T(8,128)S(1)}, u32[]{:S(2)}, u32[]{:S(2)}) %collective-permute-start.9) | collective-permute-done | bytes 196640 | tf_op jit(solution)/shard_map/ppermute | solution.py:383
  75.1 1.7 %convolution_select_fusion = f32[6,4,32,256]{3,2,1,0:T(8,128)} fusion(f32[6,4,32,256]{3,2,1,0:T(8,128)S(1)} %copy-done, f32[6,4,16,128]{3,2,1,0:T(8,128)S(1)} %get-tuple-element.22, f32[6,4,16,128]{3,2,1,0:T(8,128)S(1)} %get-tuple-element.21, pred[]{:T(512)S(6)} %eq.23, f32[4,128]{1,0:T(4,128)S(1)} %pad_maximum_fusion, f32[256,64]{1,0:T(8,128)S(1)} %get-tuple-element.24, ...), kind=kOutput, calls=%fused_computation | convolution fusion | flops 302415872 | bytes 2099201 | tf_op jit(solution)/shard_map/vizk,tk->vizt/dot_general | solution.py:427
  (23 shorter events, 0.2 us)
Async XLA Ops:
  2.5 42.9 %collective-permute-start.4 = (f32[7,3,32,256]{3,2,1,0:T(8,128)}, f32[7,3,32,256]{3,2,1,0:T(8,128)S(1)}, u32[]{:S(2)}, u32[]{:S(2)}) collective-permute-start(f32[7,3,32,256]{3,2,1,0:T(8,128)} %get-tuple-element.19), channel_id=1, source_target_pairs={{32,0},{64,32},{96,64},{128,96},{160,128},{192,160},{224,192},{33,... | collective-permute-start | bytes 2064392 | tf_op jit(solution)/shard_map/ppermute | solution.py:404
  3.8 47.0 %collective-permute-start.6 = (f32[7,3,32,256]{3,2,1,0:T(8,128)}, f32[7,3,32,256]{3,2,1,0:T(8,128)S(1)}, u32[]{:S(2)}, u32[]{:S(2)}) collective-permute-start(f32[7,3,32,256]{3,2,1,0:T(8,128)} %get-tuple-element.19), channel_id=1, source_target_pairs={{0,16},{8,24},{16,0},{24,8},{1,17},{9,25},{17,1},{25,9},{2,18},{10... | collective-permute-start | bytes 2064392 | tf_op jit(solution)/shard_map/ppermute | solution.py:403
  7.8 43.1 %collective-permute-start.5 = (f32[7,3,32,256]{3,2,1,0:T(8,128)}, f32[7,3,32,256]{3,2,1,0:T(8,128)S(1)}, u32[]{:S(2)}, u32[]{:S(2)}) collective-permute-start(f32[7,3,32,256]{3,2,1,0:T(8,128)} %get-tuple-element.20), channel_id=1, source_target_pairs={{0,32},{32,64},{64,96},{96,128},{128,160},{160,192},{192,224},{1,3... | collective-permute-start | bytes 2064392 | tf_op jit(solution)/shard_map/ppermute | solution.py:409
  10.7 10.8 %collective-permute-start = (f32[28,8,256]{2,1,0:T(8,128)}, f32[28,8,256]{2,1,0:T(8,128)S(1)}, u32[]{:S(2)}, u32[]{:S(2)}) collective-permute-start(f32[28,8,256]{2,1,0:T(8,128)} %get-tuple-element.14), channel_id=1, source_target_pairs={{0,1},{1,2},{2,3},{3,4},{4,5},{5,6},{6,7},{7,0},{8,9},{9,10},{10,1... | collective-permute-start | bytes 688136 | tf_op jit(solution)/shard_map/ppermute | solution.py:411
  12.6 11.8 %collective-permute-start.1 = (f32[28,8,256]{2,1,0:T(8,128)}, f32[28,8,256]{2,1,0:T(8,128)S(1)}, u32[]{:S(2)}, u32[]{:S(2)}) collective-permute-start(f32[28,8,256]{2,1,0:T(8,128)} %get-tuple-element.15), channel_id=1, source_target_pairs={{1,0},{2,1},{3,2},{4,3},{5,4},{6,5},{7,6},{0,7},{9,8},{10,9},{11,1... | collective-permute-start | bytes 688136 | tf_op jit(solution)/shard_map/ppermute | solution.py:412
  21.5 3.5 %copy-start.4 = (f32[28,8,256]{2,1,0:T(8,128)}, f32[28,8,256]{2,1,0:T(8,128)S(1)}, u32[]{:S(2)}) copy-start(f32[28,8,256]{2,1,0:T(8,128)S(1)} %collective-permute-done.before_ref) | copy-start | bytes 688132
  21.5 15.7 %collective-permute-start.2 = (f32[7,8,128]{2,1,0:T(8,128)}, f32[7,8,128]{2,1,0:T(8,128)S(1)}, u32[]{:S(2)}, u32[]{:S(2)}) collective-permute-start(f32[7,8,128]{2,1,0:T(8,128)} %get-tuple-element.17), channel_id=1, source_target_pairs={{0,8},{8,16},{16,24},{24,0},{1,9},{9,17},{17,25},{25,1},{2,10},{10... | collective-permute-start | bytes 86024 | tf_op jit(solution)/shard_map/ppermute | solution.py:407
  24.4 0.7 copy-start.5
  24.4 14.6 %collective-permute-start.3 = (f32[7,8,128]{2,1,0:T(8,128)}, f32[7,8,128]{2,1,0:T(8,128)S(1)}, u32[]{:S(2)}, u32[]{:S(2)}) collective-permute-start(f32[7,8,128]{2,1,0:T(8,128)} %get-tuple-element.18), channel_id=1, source_target_pairs={{8,0},{16,8},{24,16},{0,24},{9,1},{17,9},{25,17},{1,25},{10,2},{18... | collective-permute-start | bytes 86024 | tf_op jit(solution)/shard_map/ppermute | solution.py:408
  37.2 1.8 %copy-start.6 = (f32[7,8,128]{2,1,0:T(8,128)}, f32[7,8,128]{2,1,0:T(8,128)S(1)}, u32[]{:S(2)}) copy-start(f32[7,8,128]{2,1,0:T(8,128)S(1)} %collective-permute-done.2.before_ref) | copy-start | bytes 86020
  39.0 0.6 copy-start.7
  45.5 0.9 %copy-start.1 = (f32[7,3,32,256]{3,2,1,0:T(8,128)}, f32[7,3,32,256]{3,2,1,0:T(8,128)S(1)}, u32[]{:S(2)}) copy-start(f32[7,3,32,256]{3,2,1,0:T(8,128)S(1)} %collective-permute-done.4.halo_ref) | copy-start | bytes 2064388
  50.9 0.9 %copy-start.2 = (f32[7,3,32,256]{3,2,1,0:T(8,128)}, f32[7,3,32,256]{3,2,1,0:T(8,128)S(1)}, u32[]{:S(2)}) copy-start(f32[7,3,32,256]{3,2,1,0:T(8,128)S(1)} %collective-permute-done.6.mirror_ref) | copy-start | bytes 2064388
  51.7 0.8 %copy-start.3 = (f32[7,3,32,256]{3,2,1,0:T(8,128)}, f32[7,3,32,256]{3,2,1,0:T(8,128)S(1)}, u32[]{:S(2)}) copy-start(f32[7,3,32,256]{3,2,1,0:T(8,128)S(1)} %collective-permute-done.5.halo_ref) | copy-start | bytes 2064388
  59.3 3.3 %collective-permute-start.7 = (f32[6,4,16,128]{3,2,1,0:T(8,128)S(1)}, f32[6,4,16,128]{3,2,1,0:T(8,128)S(1)}, u32[]{:S(2)}, u32[]{:S(2)}) collective-permute-start(f32[6,4,16,128]{3,2,1,0:T(8,128)S(1)} %slice_select_fusion), channel_id=1, source_target_pairs={{0,8},{8,0},{16,24},{24,16},{1,9},{9,1},{17,25},{25,17},{2,10},{10... | collective-permute-start | bytes 589832 | tf_op jit(solution)/shard_map/ppermute | solution.py:381
  62.7 11.3 %copy-start.8 = (s32[4]{0:T(128)S(1)}, s32[4]{0:T(128)}, u32[]{:S(2)}) copy-start(s32[4]{0:T(128)} %param.7) | copy-start | bytes 52
  62.7 12.4 %copy-start = (f32[6,4,32,256]{3,2,1,0:T(8,128)S(1)}, f32[6,4,32,256]{3,2,1,0:T(8,128)}, u32[]{:S(2)}) copy-start(f32[6,4,32,256]{3,2,1,0:T(8,128)} %shard_map.47) | copy-start | bytes 2359300
  62.7 8.3 %collective-permute-start.8 = (f32[6,4,16,128]{3,2,1,0:T(8,128)S(1)}, f32[6,4,16,128]{3,2,1,0:T(8,128)S(1)}, u32[]{:S(2)}, u32[]{:S(2)}) collective-permute-start(f32[6,4,16,128]{3,2,1,0:T(8,128)S(1)} %select_add_fusion), channel_id=1, source_target_pairs={{0,16},{16,0},{8,24},{24,8},{1,17},{17,1},{9,25},{25,9},{2,18},{18... | collective-permute-start | bytes 589832 | tf_op jit(solution)/shard_map/ppermute | solution.py:382
  71.1 4.0 %collective-permute-start.9 = (f32[6,4,16,128]{3,2,1,0:T(8,128)S(1)}, f32[6,4,16,128]{3,2,1,0:T(8,128)S(1)}, u32[]{:S(2)}, u32[]{:S(2)}) collective-permute-start(f32[6,4,16,128]{3,2,1,0:T(8,128)S(1)} %add.31), channel_id=1, source_target_pairs={{0,8},{8,0},{16,24},{24,16},{1,9},{9,1},{17,25},{25,17},{2,10},{10... | collective-permute-start | bytes 589832 | tf_op jit(solution)/shard_map/ppermute | solution.py:383
